TPU v7x, 32 devices: a whole 2x2x4 slice. The times are simulated.
32 devices in a mesh: dp: 8 (over y, x, core), seq: 4 (over z).
Axes of the slice: x: 2, y: 2, z: 4, core: 2. Of those that a mesh axis runs over, the one named last changes fastest.
Arguments:
- tile_tokens: bfloat16 [8, 128, 3200], P('dp', 'seq'), may hold values from -6 to 6
- proj_weight: bfloat16 [3200, 8192], P('dp', 'seq')
- text_hidden: bfloat16 [8, 512, 8192], P('dp', 'seq'), may hold values from -6 to 6
- cotangent: bfloat16 [8, 512, 8192], P('dp', 'seq'), may hold values from -1.1953125 to 1.1953125
- norm_gain: float32 [8192], replicated, may hold values from 0.25 to 1.75
- placeholders: int32 [8, 128], P('dp'), may hold values from 0 to 511, as said below
- bucket_levels: int32 [8, 4, 3200], P('dp', 'seq'), may hold values from 2 to 16
- row_draws: float32 [8, 4, 3200], P('dp', 'seq'), may hold values from 0 to 1
- column_draws: float32 [8, 8192], P('dp', 'seq'), may hold values from 0 to 1
Outputs:
- weight_grad: float32 [3200, 8192], P('dp', 'seq')
- gain_grad: float32 [8192], replicated
Inputs may be any that keep to these rules, and one draw needn't show every extreme that they name: Each row is strictly increasing. Among the positions of one device's block of 128 positions stand at most 48 placeholders, and in every row some block holds exactly 48.
All inputs are finite; a program needn't handle non-finite values.
Results may differ from a plain program's by a relative error of at most 0.014.
Values may be sent and summed in bfloat16 or wider, within the bound.
No kernel may reach another device: no remote copies, remote signals or barrier semaphores. Data moves between devices by JAX's collectives and lax.ppermute only.
A program may use at most 64 MiB of HBM per device.

v0:
```python
import jax
import jax.numpy as jnp
from jax import lax
from jax.sharding import PartitionSpec as P

IMG_MOST = 48
EPSILON = 1e-06


def quantize(gradient, levels_now, rows_now, columns_now):
    bucket_norm = jnp.sqrt(jnp.sum(gradient * gradient, axis=1, keepdims=True) + EPSILON)
    step_count = levels_now.astype(jnp.float32)[:, None]
    offset = 0.25 + 0.25 * (rows_now[:, None] + columns_now[None, :])
    ratio = jnp.abs(gradient) / bucket_norm * step_count
    lower = jnp.floor(ratio)
    quantum = lower + jnp.clip(2.0 * (ratio - lower - offset) + 0.5, 0.0, 1.0)
    return jnp.sign(gradient) * bucket_norm * quantum / step_count


def on_device(
    tile_tokens,
    proj_weight,
    text_hidden,
    cotangent,
    norm_gain,
    placeholders,
    bucket_levels,
    row_draws,
    column_draws,
):
    seq_count = lax.axis_size("seq")
    seq_index = lax.axis_index("seq")
    replicas = lax.axis_size("dp")
    places = placeholders[0]
    image_total = places.shape[0]
    tok_rows = text_hidden.shape[1]
    model_width = text_hidden.shape[2]
    columns = proj_weight.shape[1]
    all_positions = tok_rows * seq_count
    zero_half = jnp.zeros((), jnp.bfloat16)
    own_text = text_hidden[0]
    own_cot = cotangent[0]
    gathered = lax.all_gather(tile_tokens[0], "seq", axis=0, tiled=True)
    patch_block = gathered
    embedded = jnp.dot(
        patch_block,
        lax.all_gather(proj_weight, "dp", axis=0, tiled=True),
        preferred_element_type=jnp.float32,
    ).astype(jnp.bfloat16)
    image_marks = jnp.zeros((all_positions,), jnp.int32).at[places].set(1)
    local_marks = lax.dynamic_slice_in_dim(image_marks, seq_index * tok_rows, tok_rows)
    is_image = local_marks[:, None] == 1
    owners = places // tok_rows
    owner_ids = jnp.arange(seq_count, dtype=jnp.int32)
    counts = jnp.sum((owners[:, None] == owner_ids[None, :]).astype(jnp.int32), axis=0)
    starts = jnp.cumsum(counts) - counts
    own_start = starts[seq_index]
    own_count = counts[seq_index]
    slot_ids = jnp.arange(IMG_MOST, dtype=jnp.int32)
    source_rows = jnp.clip(own_start + slot_ids, 0, image_total - 1)
    local_slots = jnp.clip(jnp.take(places, source_rows) - seq_index * tok_rows, 0, tok_rows - 1)
    slot_live = (slot_ids < own_count)[:, None]
    flat_index = owners * IMG_MOST + (
        jnp.arange(image_total, dtype=jnp.int32) - jnp.take(starts, owners)
    )
    outgoing = jnp.where(slot_live, jnp.take(own_cot, local_slots, axis=0), zero_half)
    returned = lax.all_to_all(outgoing[None], "seq", split_axis=2, concat_axis=0, tiled=True)
    image_cot = jnp.take(returned.reshape(-1, columns), flat_index, axis=0).astype(jnp.float32)
    emb_float = embedded.astype(jnp.float32)
    column_gain = lax.dynamic_slice_in_dim(norm_gain, seq_index * columns, columns)
    grad_in = image_cot * column_gain[None, :]
    squares, mixed = lax.psum(
        (jnp.sum(emb_float * emb_float, axis=1), jnp.sum(grad_in * emb_float, axis=1)), "seq"
    )
    inverse = lax.rsqrt(squares / model_width + EPSILON)[:, None]
    normed = emb_float * inverse
    emb_grad = ((grad_in - normed * (mixed[:, None] * inverse / model_width)) * inverse).astype(
        jnp.bfloat16
    )
    image_part = jnp.sum(image_cot * normed, axis=0)
    text_float = own_text.astype(jnp.float32)
    text_inverse = lax.rsqrt(jnp.mean(text_float * text_float, axis=1, keepdims=True) + EPSILON)
    text_terms = own_cot.astype(jnp.float32) * text_float * text_inverse
    text_part = jnp.sum(jnp.where(is_image, 0.0, text_terms), axis=0)
    placed_part = lax.dynamic_update_slice_in_dim(
        jnp.zeros((model_width,), jnp.float32), image_part, seq_index * columns, 0
    )
    gain_part = text_part + placed_part
    own_levels = bucket_levels[0, 0]
    own_row_draws = row_draws[0, 0]
    own_column_draws = column_draws[0]
    patch_block = gathered
    gradient = lax.dot_general(
        patch_block, emb_grad, (((0,), (0,)), ((), ())), preferred_element_type=jnp.float32
    )
    summed = lax.psum_scatter(
        quantize(gradient, own_levels, own_row_draws, own_column_draws).astype(jnp.bfloat16),
        "dp",
        scatter_dimension=0,
        tiled=True,
    ).astype(jnp.float32)
    gain_total = lax.psum(gain_part, ("dp", "seq"))
    return (summed / replicas, gain_total / replicas)


def solution(mesh):
    return jax.shard_map(
        on_device,
        mesh=mesh,
        in_specs=(
            P("dp", "seq", None),
            P("dp", "seq"),
            P("dp", "seq", None),
            P("dp", "seq", None),
            P(),
            P("dp", None),
            P("dp", "seq", None),
            P("dp", "seq", None),
            P("dp", "seq"),
        ),
        out_specs=(P("dp", "seq"), P()),
        check_vma=False,
    )
```

profile of v0, /device:TPU:0, one launch (start us, length us, event | category | flops | bytes accessed | tf_op | source)
XLA Modules:
  0.0 315.0 jit_solution(2458585537406789046)
XLA Ops:
  7.2 0.0 copy-start
  7.2 0.0 all-gather.3.cloned.1.call-start
  7.3 0.7 all-gather.3.cloned.1.call-update
  7.9 0.7 and_select_fusion.5
  8.6 0.1 convert_reduce_fusion.1
  8.7 0.2 reduce-window.9
  8.9 0.6 dynamic_slice.12
  9.5 0.7 fusion.34
  10.2 0.7 fusion.33
  10.9 1.4 gather_fusion
  12.3 0.7 fusion.31
  13.0 3.6 %gather_fusion.1 = bf16[48,8192]{1,0:T(8,128)(2,1)S(1)} fusion(bf16[128,8192]{1,0:T(8,128)(2,1)} %bitcast.74, s32[1024]{0:T(1024)S(1)} %pad_clamp_fusion.1), kind=kCustom, calls=%fused_computation.1 | custom fusion | bytes 1573056 | tf_op jit(solution)/shard_map/jit(_take)/gather | solution.py:66
  16.6 1.3 compare_and_fusion
  17.9 0.2 fusion.21
  18.1 6.8 %copy.22 = bf16[1,48,8192]{1,0,2:T(2,128)(2,1)} copy(bf16[1,48,8192]{2,1,0:T(8,128)(2,1)S(1)} %fusion.21) | data formatting | bytes 1572864 | tf_op jit(solution)/shard_map/jit(_where)/select_n | solution.py:66
  24.8 0.5 broadcast.575
  25.3 45.2 %reduce.4 = bf16[8192,48]{1,0:T(8,128)(2,1)S(1)} reduce(bf16[8192,1,48]{2,1,0:T(2,128)(2,1)} %bitcast.76, bf16[]{:T(256)} %broadcast.575), dimensions={1}, to_apply=%bitcast.63.reduce_sub_computation | reduce | bytes 1572866
  70.6 4.0 %reshape.423 = bf16[4,2,49152]{2,1,0:T(2,128)(2,1)} reshape(bf16[8192,48]{1,0:T(8,128)(2,1)S(1)} %reduce.4) | data formatting | bytes 1572864
  74.6 6.3 %all-to-all-start = ((bf16[4,2,49152]{2,1,0:T(2,128)(2,1)}), bf16[4,2,49152]{2,1,0:T(2,128)(2,1)S(1)}, u32[]{:S(2)}, u32[]{:S(2)}) async-start(bf16[4,2,49152]{2,1,0:T(2,128)(2,1)} %reshape.423), calls=%async_computation | async-start | bytes 1572864 | tf_op jit(solution)/shard_map/all_to_all | solution.py:67
  80.9 0.7 dynamic_slice.14
  81.7 2.6 compare_and_fusion.1
  84.4 30.7 %all-gather = bf16[1,128,3200]{2,1,0:T(8,128)(2,1)S(1)} all-gather(bf16[1,32,3200]{2,1,0:T(8,128)(2,1)S(1)} %copy-done.4), channel_id=2, replica_groups=mesh['dp'=8,'seq'=4] {'seq'}, dimensions={1}, use_global_device_ids=true | all-gather | bytes 1024000 | tf_op jit(solution)/shard_map/all_gather | solution.py:43
  115.0 4.6 %reshape.424 = bf16[8192,1,48]{2,1,0:T(2,128)(2,1)} reshape(bf16[4,2,49152]{2,1,0:T(2,128)(2,1)S(1)} %all-to-all-done) | data formatting | bytes 1572864
  119.6 8.1 %copy.23 = bf16[1,48,8192]{2,1,0:T(8,128)(2,1)S(1)} copy(bf16[1,48,8192]{1,0,2:T(2,128)(2,1)} %bitcast.77) | data formatting | bytes 1572864 | tf_op jit(solution)/shard_map/all_to_all | solution.py:67
  127.8 0.6 all_to_all.12
  128.4 0.4 copy.24
  128.8 0.9 gather_fusion.2
  129.8 0.0 all-gather.3.cloned.1.call-done
  129.8 7.1 %multiply_reduce_fusion.1 = (f32[128]{0:T(128)S(1)}, f32[128,2048]{1,0:T(8,128)S(1)}) fusion(bf16[3200,2048]{1,0:T(8,128)(2,1)} %all-gather.3.cloned.1.call-done, bf16[1,128,3200]{2,1,0:T(8,128)(2,1)S(1)} %all-gather), kind=kOutput, calls=%fused_computation.31 | convolution fusion | flops 1678770048 | bytes 14975488 | tf_op jit(solution)/shard_map/dot_general | solution.py:45
  136.8 0.0 copy-start.2
  136.9 11.1 %psum.21 = f32[128]{0:T(128)S(1)} all-reduce(f32[128]{0:T(128)S(1)} %get-tuple-element.22), channel_id=1, replica_groups=mesh['dp'=8,'seq'=4] {'seq'}, use_global_device_ids=true, to_apply=%region_3.4 | all-reduce | flops 128 | bytes 1024 | tf_op jit(solution)/shard_map/psum | solution.py:72
  148.0 0.4 fusion.17
  148.4 8.4 %psum.22 = f32[128]{0:T(128)S(1)} all-reduce(f32[128]{0:T(128)S(1)} %get-tuple-element.13), channel_id=1, replica_groups=mesh['dp'=8,'seq'=4] {'seq'}, use_global_device_ids=true, to_apply=%region_5.6 | all-reduce | flops 128 | bytes 1024 | tf_op jit(solution)/shard_map/psum | solution.py:72
  156.8 0.0 copy-start.7
  156.8 5.1 %multiply_reduce_fusion = (f32[3200]{0:T(1024)S(1)}, f32[2048,3200]{1,0:T(8,128)S(1)}) fusion(bf16[1,128,3200]{2,1,0:T(8,128)(2,1)S(1)} %all-gather, f32[128,2048]{1,0:T(8,128)} %copy-done.2, f32[128]{0:T(128)S(1)} %multiply_multiply_fusion, f32[128]{0:T(128)S(1)} %add_rsqrt_fusion.1, f32[2048]{0:T(1024)S(1)} %dynamic_slice.14, ...), kind=kOutput, calls=%fused_computation.12 | convolution fusion | flops 1692922752 | bytes 28628608 | tf_op jit(solution)/shard_map/dot_general | solution.py:93
  162.0 22.2 %fusion.6 = bf16[3200,2048]{0,1:T(8,128)(2,1)} fusion(f32[2048,3200]{1,0:T(8,128)S(1)} %get-tuple-element.25, f32[3200]{0:T(1024)S(1)} %convert_reduce_fusion, f32[2048]{0:T(1024)S(1)} %bitcast.79, f32[3200]{0:T(1024)S(1)} %reduce.2, f32[3200]{0:T(1024)S(1)} %add_sqrt_fusion), kind=kLoop, calls=%fused_computation.13 | loop fusion | flops 117964800 | bytes 39368192 | tf_op jit(solution)/shard_map/convert_element_type | solution.py:97
  184.1 18.3 %copy.26 = bf16[3200,2048]{1,0:T(8,128)(2,1)} copy(bf16[3200,2048]{0,1:T(8,128)(2,1)} %fusion.6) | data formatting | bytes 26214400
  202.5 0.0 reduce-scatter.4.cloned.1.call-update
  202.5 1.0 scatter_custom_fusion
  203.5 0.1 dynamic-slice_compare_fusion
  203.6 2.1 fusion.10
  205.7 2.6 fusion.9
  208.3 41.3 %psum.23 = f32[8192]{0:T(1024)S(1)} all-reduce(f32[8192]{0:T(1024)S(1)} %add_dynamic-update-slice_fusion), channel_id=1, replica_groups=mesh['dp'=8,'seq'=4] {'dp','seq'}, use_global_device_ids=true, to_apply=%region_12.13 | all-reduce | flops 8192 | bytes 65536 | tf_op jit(solution)/shard_map/psum | solution.py:102
  249.7 0.6 broadcast_multiply_fusion
  250.3 47.4 %reduce-scatter.4.cloned.1.call-done = bf16[400,2048]{1,0:T(8,128)(2,1)} async-done(((bf16[3200,2048]{1,0:T(8,128)(2,1)}), bf16[400,2048]{1,0:T(8,128)(2,1)}) %reduce-scatter.4.cloned.1.call-update) | async-done | bytes 1638416
  297.7 2.8 copy.27
  300.5 2.5 convert_multiply_fusion.2
  303.0 5.2 %copy.25 = f32[400,2048]{1,0:T(8,128)} copy(f32[400,2048]{0,1:T(8,128)} %convert_multiply_fusion.2) | data formatting | bytes 6553600
  (29 shorter events, 0.2 us)
Async XLA Ops:
  7.2 74.5 %copy-start = (s32[1,128]{1,0:T(1,128)S(1)}, s32[1,128]{1,0:T(1,128)}, u32[]{:S(2)}) copy-start(s32[1,128]{1,0:T(1,128)} %param.14) | copy-start | bytes 1540
  7.2 74.5 %copy-start.6 = (f32[1,1,3200]{2,1,0:T(1,128)S(1)}, f32[1,1,3200]{2,1,0:T(1,128)}, u32[]{:S(2)}) copy-start(f32[1,1,3200]{2,1,0:T(1,128)} %param.16) | copy-start | bytes 38404
  7.2 77.1 %copy-start.5 = (s32[1,1,3200]{2,1,0:T(1,128)S(1)}, s32[1,1,3200]{2,1,0:T(1,128)}, u32[]{:S(2)}) copy-start(s32[1,1,3200]{2,1,0:T(1,128)} %param.15) | copy-start | bytes 38404
  7.2 77.2 %copy-start.4 = (bf16[1,32,3200]{2,1,0:T(8,128)(2,1)S(1)}, bf16[1,32,3200]{2,1,0:T(8,128)(2,1)}, u32[]{:S(2)}) copy-start(bf16[1,32,3200]{2,1,0:T(8,128)(2,1)} %param.9) | copy-start | bytes 614404
  7.2 122.6 %all-gather.3.cloned.1.call-start = ((), (), s32[]{:S(2)}) async-start(), calls=%async_computation.2 | async-start | bytes 14745600 | tf_op jit(solution)/shard_map/all_gather | solution.py:47
  74.6 40.5 %all-to-all-start = ((bf16[4,2,49152]{2,1,0:T(2,128)(2,1)}), bf16[4,2,49152]{2,1,0:T(2,128)(2,1)S(1)}, u32[]{:S(2)}, u32[]{:S(2)}) async-start(bf16[4,2,49152]{2,1,0:T(2,128)(2,1)} %reshape.423), calls=%async_computation | async-start | bytes 1572864 | tf_op jit(solution)/shard_map/all_to_all | solution.py:67
  80.9 216.8 %reduce-scatter.4.cloned.1.call-start = ((), (), s32[]{:S(2)}) async-start(), calls=%async_computation.3 | async-start | bytes 14745600
  129.7 27.0 %copy-start.3 = (bf16[128,2048]{1,0:T(8,128)(2,1)}, bf16[128,2048]{1,0:T(8,128)(2,1)S(1)}, u32[]{:S(2)}) copy-start(bf16[128,2048]{1,0:T(8,128)(2,1)S(1)} %gather_fusion.2) | copy-start | bytes 1572868
  136.8 19.9 %copy-start.2 = (f32[128,2048]{1,0:T(8,128)}, f32[128,2048]{1,0:T(8,128)S(1)}, u32[]{:S(2)}) copy-start(f32[128,2048]{1,0:T(8,128)S(1)} %get-tuple-element.23) | copy-start | bytes 3145732
  156.8 5.2 %copy-start.7 = (f32[1,2048]{1,0:T(1,128)S(1)}, f32[1,2048]{1,0:T(1,128)}, u32[]{:S(2)}) copy-start(f32[1,2048]{1,0:T(1,128)} %param.17) | copy-start | bytes 24580
  202.5 3.2 %copy-start.1 = (bf16[1,128,8192]{2,1,0:T(8,128)(2,1)S(1)}, bf16[1,128,8192]{2,1,0:T(8,128)(2,1)}, u32[]{:S(2)}) copy-start(bf16[1,128,8192]{2,1,0:T(8,128)(2,1)} %param.12) | copy-start | bytes 6291460
Sparse Core Ops, SparseCore 0:
  9.9 76.9 all-gather.2
  202.6 95.0 reduce-scatter.3
where the time goes:
time: 316 us; the launch traced here: 315 us
  blocking collectives  91.5 us (29%)
  other arithmetic  82.2 us (26%)
  local copies, waits for them, and re-layouts  60.3 us (19%)
  waiting for transfers between devices  48.1 us (15%)
  between operations  14.3 us (5%)
  matrix products  12.2 us (4%)
  starting transfers between devices  6.39 us (2%)
    unnamed x3, waiting for transfers between devices  48.1 us
    unnamed x2, other arithmetic  45.3 us
    psum x1, blocking collectives, on_device(): gain_total = lax.psum(gain_part, ('dp', 'seq'))  41.3 us
    unnamed x22, local copies, waits for them, and re-layouts  35.4 us
    all_gather x1, blocking collectives, on_device(): gathered = lax.all_gather(tile_tokens[0], 'seq', axis=0, tiled=True)  30.7 us
    convert_element_type x1, other arithmetic, on_device(): quantize(gradient, own_levels, own_row_draws, own_column_draws)  22.2 us
    psum x2, blocking collectives, on_device(): lax.psum((jnp.sum(emb_float * emb_float, axis=1), jnp.sum(grad_in * emb_f...  19.5 us
    all_to_all x3, local copies, waits for them, and re-layouts, on_device(): lax.all_to_all(outgoing[None], 'seq', split_axis=2, concat_axis=0, tiled=...  9.14 us
  transfers between devices with their start and end apart: 3, of which 1 were waited for; matrix products, arithmetic and copies ran while one was open for 29% of the time, Pallas kernels for 0%

commit v1 on v0

--- a/solution.py
+++ b/solution.py
@@ -99,7 +99,7 @@
         scatter_dimension=0,
         tiled=True,
     ).astype(jnp.float32)
-    gain_total = lax.psum(gain_part, ("dp", "seq"))
+    gain_total = lax.psum(lax.psum(gain_part, "dp"), "seq")
     return (summed / replicas, gain_total / replicas)
 
 

time: 316 us -> 354 us (1.12)
  waiting for transfers between devices: 48.1 us -> 93.5 us
  blocking collectives: 91.5 us -> 77.2 us
  local copies, waits for them, and re-layouts: 60.3 us -> 64.8 us
    unnamed x3, waiting for transfers between devices: 48.1 us -> 93.5 us
    psum x1, blocking collectives: 41.3 us -> 22.4 us  [on_device(): gain_total = lax.psum(lax.psum(gain_part, 'dp'), 'seq')]
    psum x2, blocking collectives: 19.5 us -> 27.4 us  [on_device(): lax.psum((jnp.sum(emb_float * emb_float, axis=1), jnp.sum(grad_in * emb_f...]
  transfers between devices with their start and end apart: 3 -> 3, of which waited for: 1 -> 1; matrix products, arithmetic and copies ran while one was open for 29% -> 27% of each run, Pallas kernels for 0% -> 0%
where the time goes in v1:
time: 354 us; the launch traced here: 352 us
  waiting for transfers between devices  93.5 us (26%)
  other arithmetic  84 us (24%)
  blocking collectives  77.2 us (22%)
  local copies, waits for them, and re-layouts  64.8 us (18%)
  between operations  14.3 us (4%)
  matrix products  12 us (3%)
  starting transfers between devices  6.49 us (2%)
    unnamed x3, waiting for transfers between devices  93.5 us
    unnamed x2, other arithmetic  46.5 us
    unnamed x22, local copies, waits for them, and re-layouts  37.7 us
    all_gather x1, blocking collectives, on_device(): gathered = lax.all_gather(tile_tokens[0], 'seq', axis=0, tiled=True)  27.5 us
    psum x2, blocking collectives, on_device(): lax.psum((jnp.sum(emb_float * emb_float, axis=1), jnp.sum(grad_in * emb_f...  27.4 us
    psum x1, blocking collectives, on_device(): gain_total = lax.psum(lax.psum(gain_part, 'dp'), 'seq')  22.4 us
    convert_element_type x1, other arithmetic, on_device(): quantize(gradient, own_levels, own_row_draws, own_column_draws)  22.1 us
    all_to_all x3, local copies, waits for them, and re-layouts, on_device(): lax.all_to_all(outgoing[None], 'seq', split_axis=2, concat_axis=0, tiled=...  9.14 us
  transfers between devices with their start and end apart: 3, of which 1 were waited for; matrix products, arithmetic and copies ran while one was open for 27% of the time, Pallas kernels for 0%

profile of v1, /device:TPU:0, one launch (start us, length us, event | category | flops | bytes accessed | tf_op | source)
XLA Modules:
  0.0 352.4 jit_solution(5504778816163240057)
XLA Ops:
  7.2 0.0 copy-start
  7.2 0.0 all-gather.3.cloned.1.call-start
  7.2 0.7 all-gather.3.cloned.1.call-update
  7.9 0.7 and_select_fusion.5
  8.6 0.1 convert_reduce_fusion.1
  8.7 0.6 dynamic_slice.12
  9.3 0.2 reduce-window.9
  9.5 0.6 fusion.34
  10.2 0.7 fusion.33
  10.8 1.4 gather_fusion
  12.3 0.7 fusion.31
  13.0 0.0 copy-start.4
  13.0 3.8 %gather_fusion.1 = bf16[48,8192]{1,0:T(8,128)(2,1)S(1)} fusion(bf16[128,8192]{1,0:T(8,128)(2,1)} %bitcast.75, s32[1024]{0:T(1024)S(1)} %pad_clamp_fusion.1), kind=kCustom, calls=%fused_computation.1 | custom fusion | bytes 1573056 | tf_op jit(solution)/shard_map/jit(_take)/gather | solution.py:66
  16.8 1.3 compare_and_fusion
  18.0 1.0 fusion.21
  19.1 8.9 %copy.22 = bf16[1,48,8192]{1,0,2:T(2,128)(2,1)} copy(bf16[1,48,8192]{2,1,0:T(8,128)(2,1)} %fusion.21) | data formatting | bytes 1572864 | tf_op jit(solution)/shard_map/jit(_where)/select_n | solution.py:66
  28.0 0.5 broadcast.575
  28.5 46.5 %reduce.4 = bf16[8192,48]{1,0:T(8,128)(2,1)} reduce(bf16[8192,1,48]{2,1,0:T(2,128)(2,1)} %bitcast.77, bf16[]{:T(256)} %broadcast.575), dimensions={1}, to_apply=%bitcast.63.reduce_sub_computation | reduce | bytes 1572866
  74.9 5.1 %reshape.423 = bf16[4,2,49152]{2,1,0:T(2,128)(2,1)} reshape(bf16[8192,48]{1,0:T(8,128)(2,1)} %reduce.4) | data formatting | bytes 1572864
  80.0 6.5 %all-to-all-start = ((bf16[4,2,49152]{2,1,0:T(2,128)(2,1)}), bf16[4,2,49152]{2,1,0:T(2,128)(2,1)}, u32[]{:S(2)}, u32[]{:S(2)}) async-start(bf16[4,2,49152]{2,1,0:T(2,128)(2,1)} %reshape.423), calls=%async_computation | async-start | bytes 1572864 | tf_op jit(solution)/shard_map/all_to_all | solution.py:67
  86.5 1.0 scatter_custom_fusion
  87.5 2.5 compare_and_fusion.1
  90.0 0.1 dynamic-slice_compare_fusion
  90.1 0.7 dynamic_slice.14
  90.9 2.1 fusion.10
  93.0 27.5 %all-gather = bf16[1,128,3200]{2,1,0:T(8,128)(2,1)S(1)} all-gather(bf16[1,32,3200]{2,1,0:T(8,128)(2,1)S(1)} %copy-done.4), channel_id=2, replica_groups=mesh['dp'=8,'seq'=4] {'seq'}, dimensions={1}, use_global_device_ids=true | all-gather | bytes 1024000 | tf_op jit(solution)/shard_map/all_gather | solution.py:43
  120.5 2.5 fusion.9
  123.0 5.8 %reshape.424 = bf16[8192,1,48]{2,1,0:T(2,128)(2,1)} reshape(bf16[4,2,49152]{2,1,0:T(2,128)(2,1)} %all-to-all-done) | data formatting | bytes 1572864
  128.8 8.1 %copy.23 = bf16[1,48,8192]{2,1,0:T(8,128)(2,1)S(1)} copy(bf16[1,48,8192]{1,0,2:T(2,128)(2,1)} %bitcast.78) | data formatting | bytes 1572864 | tf_op jit(solution)/shard_map/all_to_all | solution.py:67
  136.9 0.6 all_to_all.12
  137.5 0.4 copy.24
  137.9 0.9 gather_fusion.2
  138.9 0.0 all-gather.3.cloned.1.call-done
  138.9 6.9 %multiply_reduce_fusion.1 = (f32[128]{0:T(128)S(1)}, f32[128,2048]{1,0:T(8,128)S(1)}) fusion(bf16[3200,2048]{1,0:T(8,128)(2,1)} %all-gather.3.cloned.1.call-done, bf16[1,128,3200]{2,1,0:T(8,128)(2,1)S(1)} %all-gather), kind=kOutput, calls=%fused_computation.31 | convolution fusion | flops 1678770048 | bytes 14975488 | tf_op jit(solution)/shard_map/dot_general | solution.py:45
  145.8 11.1 %psum.28 = f32[128]{0:T(128)S(1)} all-reduce(f32[128]{0:T(128)S(1)} %get-tuple-element.24), channel_id=1, replica_groups=mesh['dp'=8,'seq'=4] {'seq'}, use_global_device_ids=true, to_apply=%region_3.4 | all-reduce | flops 128 | bytes 1024 | tf_op jit(solution)/shard_map/psum | solution.py:72
  157.0 0.4 fusion.17
  157.4 22.4 %psum.30 = f32[8192]{0:T(1024)S(1)} all-reduce(f32[8192]{0:T(1024)S(1)} %add_dynamic-update-slice_fusion), channel_id=1, replica_groups=mesh['dp'=8,'seq'=4] {'dp'}, use_global_device_ids=true, to_apply=%region_12.13 | all-reduce | flops 8192 | bytes 65536 | tf_op jit(solution)/shard_map/psum | solution.py:102
  179.8 16.3 %all-reduce = (f32[128]{0:T(128)S(1)}, f32[8192]{0:T(1024)S(1)}) all-reduce(f32[128]{0:T(128)S(1)} %get-tuple-element.13, f32[8192]{0:T(1024)S(1)} %psum.30), channel_id=1, replica_groups=mesh['dp'=8,'seq'=4] {'seq'}, use_global_device_ids=true, to_apply=%region_5.6 | all-reduce | flops 8320 | bytes 66560 | tf_op jit(solution)/shard_map/psum | solution.py:72
  196.1 0.0 copy-start.7
  196.1 5.1 %multiply_reduce_fusion = (f32[3200]{0:T(1024)S(1)}, f32[2048,3200]{1,0:T(8,128)S(1)}) fusion(bf16[1,128,3200]{2,1,0:T(8,128)(2,1)S(1)} %all-gather, f32[128,2048]{1,0:T(8,128)} %copy-done.2, f32[128]{0:T(128)S(1)} %multiply_multiply_fusion, f32[128]{0:T(128)S(1)} %add_rsqrt_fusion.1, f32[2048]{0:T(1024)S(1)} %dynamic_slice.14, ...), kind=kOutput, calls=%fused_computation.12 | convolution fusion | flops 1692922752 | bytes 28628608 | tf_op jit(solution)/shard_map/dot_general | solution.py:93
  201.2 22.1 %fusion.6 = bf16[3200,2048]{0,1:T(8,128)(2,1)} fusion(f32[2048,3200]{1,0:T(8,128)S(1)} %get-tuple-element.27, f32[3200]{0:T(1024)S(1)} %convert_reduce_fusion, f32[2048]{0:T(1024)S(1)} %bitcast.80, f32[3200]{0:T(1024)S(1)} %reduce.2, f32[3200]{0:T(1024)S(1)} %add_sqrt_fusion), kind=kLoop, calls=%fused_computation.13 | loop fusion | flops 117964800 | bytes 39368192 | tf_op jit(solution)/shard_map/convert_element_type | solution.py:97
  223.3 18.3 %copy.26 = bf16[3200,2048]{1,0:T(8,128)(2,1)} copy(bf16[3200,2048]{0,1:T(8,128)(2,1)} %fusion.6) | data formatting | bytes 26214400
  241.7 0.0 reduce-scatter.4.cloned.1.call-update
  241.7 0.6 broadcast_multiply_fusion
  242.3 92.8 %reduce-scatter.4.cloned.1.call-done = bf16[400,2048]{1,0:T(8,128)(2,1)} async-done(((bf16[3200,2048]{1,0:T(8,128)(2,1)}), bf16[400,2048]{1,0:T(8,128)(2,1)}) %reduce-scatter.4.cloned.1.call-update) | async-done | bytes 1638416
  335.1 2.8 copy.27
  337.8 2.5 convert_multiply_fusion.2
  340.4 5.2 %copy.25 = f32[400,2048]{1,0:T(8,128)} copy(f32[400,2048]{0,1:T(8,128)} %convert_multiply_fusion.2) | data formatting | bytes 6553600
  (29 shorter events, 0.2 us)
Async XLA Ops:
  7.2 79.3 %copy-start = (s32[1,128]{1,0:T(1,128)S(1)}, s32[1,128]{1,0:T(1,128)}, u32[]{:S(2)}) copy-start(s32[1,128]{1,0:T(1,128)} %param.14) | copy-start | bytes 1540
  7.2 82.8 %copy-start.5 = (s32[1,1,3200]{2,1,0:T(1,128)S(1)}, s32[1,1,3200]{2,1,0:T(1,128)}, u32[]{:S(2)}) copy-start(s32[1,1,3200]{2,1,0:T(1,128)} %param.15) | copy-start | bytes 38404
  7.2 83.6 %copy-start.6 = (f32[1,1,3200]{2,1,0:T(1,128)S(1)}, f32[1,1,3200]{2,1,0:T(1,128)}, u32[]{:S(2)}) copy-start(f32[1,1,3200]{2,1,0:T(1,128)} %param.16) | copy-start | bytes 38404
  7.2 131.7 %all-gather.3.cloned.1.call-start = ((), (), s32[]{:S(2)}) async-start(), calls=%async_computation.2 | async-start | bytes 14745600 | tf_op jit(solution)/shard_map/all_gather | solution.py:47
  13.0 80.0 %copy-start.4 = (bf16[1,32,3200]{2,1,0:T(8,128)(2,1)S(1)}, bf16[1,32,3200]{2,1,0:T(8,128)(2,1)}, u32[]{:S(2)}) copy-start(bf16[1,32,3200]{2,1,0:T(8,128)(2,1)} %param.9) | copy-start | bytes 614404
  13.0 107.5 %copy-start.1 = (bf16[1,128,8192]{2,1,0:T(8,128)(2,1)S(1)}, bf16[1,128,8192]{2,1,0:T(8,128)(2,1)}, u32[]{:S(2)}) copy-start(bf16[1,128,8192]{2,1,0:T(8,128)(2,1)} %param.12) | copy-start | bytes 6291460
  80.0 42.9 %all-to-all-start = ((bf16[4,2,49152]{2,1,0:T(2,128)(2,1)}), bf16[4,2,49152]{2,1,0:T(2,128)(2,1)}, u32[]{:S(2)}, u32[]{:S(2)}) async-start(bf16[4,2,49152]{2,1,0:T(2,128)(2,1)} %reshape.423), calls=%async_computation | async-start | bytes 1572864 | tf_op jit(solution)/shard_map/all_to_all | solution.py:67
  86.5 248.6 %reduce-scatter.4.cloned.1.call-start = ((), (), s32[]{:S(2)}) async-start(), calls=%async_computation.3 | async-start | bytes 14745600
  138.9 57.2 %copy-start.3 = (bf16[128,2048]{1,0:T(8,128)(2,1)}, bf16[128,2048]{1,0:T(8,128)(2,1)S(1)}, u32[]{:S(2)}) copy-start(bf16[128,2048]{1,0:T(8,128)(2,1)S(1)} %gather_fusion.2) | copy-start | bytes 1572868
  145.8 50.2 %copy-start.2 = (f32[128,2048]{1,0:T(8,128)}, f32[128,2048]{1,0:T(8,128)S(1)}, u32[]{:S(2)}) copy-start(f32[128,2048]{1,0:T(8,128)S(1)} %get-tuple-element.25) | copy-start | bytes 3145732
  196.1 5.2 %copy-start.7 = (f32[1,2048]{1,0:T(1,128)S(1)}, f32[1,2048]{1,0:T(1,128)}, u32[]{:S(2)}) copy-start(f32[1,2048]{1,0:T(1,128)} %param.17) | copy-start | bytes 24580
Sparse Core Ops, SparseCore 0:
  9.9 76.9 all-gather.2
  241.8 93.2 reduce-scatter.3
